TPU v7x, 8 devices: a whole 2x2x1 slice. The times are simulated.
8 devices in a mesh: data: 2 (over z, y), fsdp: 2 (over x), model: 2 (over core).
Axes of the slice: x: 2, y: 2, z: 1, core: 2. Of those that a mesh axis runs over, the one named last changes fastest.
Arguments:
- x_in: bfloat16 [128, 128, 2048], P(('data', 'fsdp'), 'model')
- grad_out: bfloat16 [128, 128, 2048], P(('data', 'fsdp'), 'model')
- gain_attn: float32 [2048], replicated
- gain_mlp: float32 [2048], replicated
- w_qkv: bfloat16 [2048, 3072], P(('data', 'fsdp'), 'model')
- w_out: bfloat16 [2048, 2048], P('model', ('data', 'fsdp'))
- w_gate: bfloat16 [2048, 8192], P(('data', 'fsdp'), 'model')
- w_up: bfloat16 [2048, 8192], P(('data', 'fsdp'), 'model')
- w_down: bfloat16 [8192, 2048], P('model', ('data', 'fsdp'))
- rope_cos: float32 [128, 32], replicated
- rope_sin: float32 [128, 32], replicated
Outputs:
- output 1: bfloat16 [128, 128, 2048], P(('data', 'fsdp'), 'model')
- output 2: bfloat16 [128, 128, 2048], P(('data', 'fsdp'), 'model')
- output 3: float32 [2048, 3072], P(('data', 'fsdp'), 'model')
- output 4: float32 [2048, 2048], P('model', ('data', 'fsdp'))
- output 5: float32 [2048, 8192], P(('data', 'fsdp'), 'model')
- output 6: float32 [2048, 8192], P(('data', 'fsdp'), 'model')
- output 7: float32 [8192, 2048], P('model', ('data', 'fsdp'))
All inputs are finite; a program needn't handle non-finite values.
Results may differ from a plain program's by a relative error of at most 0.0170236.
Values are sent between devices in bfloat16 or wider.
A program may use at most 1 GiB of HBM per device.

v0:
```python
import functools
import jax
import jax.numpy as jnp
from jax import lax
from jax.sharding import PartitionSpec as P

FSDP_AXES = ('data', 'fsdp')


def rms_norm(x_f32, gain_vec):
    mean_sq = jnp.mean(x_f32 * x_f32, axis=-1, keepdims=True)
    return (x_f32 * lax.rsqrt(mean_sq + 1e-5) * gain_vec).astype(jnp.bfloat16)


def rotate_qk(qkv_proj, cos_t, sin_t):
    half_dim = qkv_proj.shape[-1] // 2
    cos_b = cos_t[None, :, None, None, :]
    sin_b = sin_t[None, :, None, None, :]
    qk_part = qkv_proj[:, :, :, :-1]
    lo_half = qk_part[..., :half_dim]
    hi_half = qk_part[..., half_dim:]
    rotated = jnp.concatenate([lo_half * cos_b - hi_half * sin_b, hi_half * cos_b + lo_half * sin_b], axis=-1).astype(jnp.bfloat16)
    return rotated[:, :, :, :-1], rotated[:, :, :, -1], qkv_proj[:, :, :, -1].astype(jnp.bfloat16)


def attention_core(q_rot, k_rot, v_val, q_start):
    score_scale = q_rot.shape[-1] ** -0.5
    scores = jnp.einsum('bskgd,btkd->bkgst', q_rot, k_rot, preferred_element_type=jnp.float32) * score_scale
    q_pos = q_start + jnp.arange(q_rot.shape[1])
    k_pos = jnp.arange(k_rot.shape[1])
    causal = q_pos[:, None] >= k_pos[None, :]
    scores = jnp.where(causal, scores, -1e30)
    attn_probs = jax.nn.softmax(scores, axis=-1).astype(jnp.bfloat16)
    attn_mix = jnp.einsum('bkgst,btkd->bskgd', attn_probs, v_val, preferred_element_type=jnp.float32)
    return attn_mix.astype(jnp.bfloat16)


def gather_rows(w_shard):
    return lax.all_gather(w_shard, FSDP_AXES, axis=0, tiled=True)


def gather_cols(w_shard):
    return lax.all_gather(w_shard, FSDP_AXES, axis=1, tiled=True)


def seq_gather(act_shard):
    return lax.all_gather(act_shard, 'model', axis=1, tiled=True)


def seq_scatter(part_sum):
    return lax.psum_scatter(part_sum, 'model', scatter_dimension=1, tiled=True)


def layer_body(x_in, grad_out, gain_attn, gain_mlp, w_qkv, w_out, w_gate, w_up, w_down, rope_cos, rope_sin):
    batch_loc = x_in.shape[0]
    seq_full = rope_cos.shape[0]
    head_dim = 2 * rope_cos.shape[1]
    qkv_width = w_qkv.shape[1]
    attn_width = w_out.shape[0]
    kv_loc = (qkv_width - attn_width) // (2 * head_dim)
    group_size = attn_width // (head_dim * kv_loc)

    x_f32 = x_in.astype(jnp.float32)
    h_attn, norm_attn_pull = jax.vjp(functools.partial(rms_norm, gain_vec=gain_attn), x_f32)
    h_attn_full = seq_gather(h_attn)
    qkv_full = gather_rows(w_qkv)
    qkv_proj = jnp.einsum('bsd,dc->bsc', h_attn_full, qkv_full, preferred_element_type=jnp.float32)
    qkv_proj = qkv_proj.reshape(batch_loc, seq_full, kv_loc, group_size + 2, head_dim)
    (q_rot, k_rot, v_val), rope_pull = jax.vjp(functools.partial(rotate_qk, cos_t=rope_cos, sin_t=rope_sin), qkv_proj)
    attn_val, attn_pull = jax.vjp(functools.partial(attention_core, q_start=0), q_rot, k_rot, v_val)
    attn_flat = attn_val.reshape(batch_loc, seq_full, attn_width)
    out_full = gather_cols(w_out)
    attn_part = jnp.einsum('bsh,hd->bsd', attn_flat, out_full, preferred_element_type=jnp.float32).astype(jnp.bfloat16)
    attn_sum = seq_scatter(attn_part)
    mid_in = (x_f32 + attn_sum.astype(jnp.float32)).astype(jnp.bfloat16).astype(jnp.float32)

    h_mlp, norm_mlp_pull = jax.vjp(functools.partial(rms_norm, gain_vec=gain_mlp), mid_in)
    h_mlp_full = seq_gather(h_mlp)
    gate_full = gather_rows(w_gate)
    up_full = gather_rows(w_up)
    gate_val = jnp.einsum('bsd,df->bsf', h_mlp_full, gate_full, preferred_element_type=jnp.float32)
    up_val = jnp.einsum('bsd,df->bsf', h_mlp_full, up_full, preferred_element_type=jnp.float32)
    gate_sig = jax.nn.sigmoid(gate_val)
    gate_act = gate_val * gate_sig
    act_val = (gate_act * up_val).astype(jnp.bfloat16)
    down_full = gather_cols(w_down)
    mlp_part = jnp.einsum('bsf,fd->bsd', act_val, down_full, preferred_element_type=jnp.float32).astype(jnp.bfloat16)
    y_out = (mid_in + seq_scatter(mlp_part).astype(jnp.float32)).astype(jnp.bfloat16)

    grad_full = seq_gather(grad_out)
    down_again = gather_cols(w_down)
    d_act = jnp.einsum('bsd,fd->bsf', grad_full, down_again, preferred_element_type=jnp.float32)
    d_act = d_act.astype(jnp.bfloat16).astype(jnp.float32)
    dw_down = lax.psum_scatter(jnp.einsum('bsf,bsd->fd', act_val, grad_full, preferred_element_type=jnp.float32),
                               FSDP_AXES, scatter_dimension=1, tiled=True)
    d_up = (d_act * gate_act).astype(jnp.bfloat16)
    d_gate = (d_act * up_val * gate_sig * (1.0 + gate_val * (1.0 - gate_sig))).astype(jnp.bfloat16)
    gate_again = gather_rows(w_gate)
    up_again = gather_rows(w_up)
    dh_mlp_part = (jnp.einsum('bsf,df->bsd', d_gate, gate_again, preferred_element_type=jnp.float32)
                   + jnp.einsum('bsf,df->bsd', d_up, up_again, preferred_element_type=jnp.float32)).astype(jnp.bfloat16)
    dw_gate = lax.psum_scatter(jnp.einsum('bsd,bsf->df', h_mlp_full, d_gate, preferred_element_type=jnp.float32),
                               FSDP_AXES, scatter_dimension=0, tiled=True)
    dw_up = lax.psum_scatter(jnp.einsum('bsd,bsf->df', h_mlp_full, d_up, preferred_element_type=jnp.float32),
                             FSDP_AXES, scatter_dimension=0, tiled=True)
    (d_mid_norm,) = norm_mlp_pull(seq_scatter(dh_mlp_part))
    d_mid = (grad_out.astype(jnp.float32) + d_mid_norm).astype(jnp.bfloat16)

    d_mid_full = seq_gather(d_mid)
    out_again = gather_cols(w_out)
    d_attn = jnp.einsum('bsd,hd->bsh', d_mid_full, out_again, preferred_element_type=jnp.float32).astype(jnp.bfloat16)
    dw_out = lax.psum_scatter(jnp.einsum('bsh,bsd->hd', attn_flat, d_mid_full, preferred_element_type=jnp.float32),
                              FSDP_AXES, scatter_dimension=1, tiled=True)
    d_q, d_k, d_v = attn_pull(d_attn.reshape(attn_val.shape))
    (d_qkv,) = rope_pull((d_q, d_k, d_v))
    d_qkv = d_qkv.astype(jnp.bfloat16).reshape(batch_loc, seq_full, qkv_width)
    qkv_again = gather_rows(w_qkv)
    dh_attn_part = jnp.einsum('bsc,dc->bsd', d_qkv, qkv_again, preferred_element_type=jnp.float32).astype(jnp.bfloat16)
    dw_qkv = lax.psum_scatter(jnp.einsum('bsd,bsc->dc', h_attn_full, d_qkv, preferred_element_type=jnp.float32),
                              FSDP_AXES, scatter_dimension=0, tiled=True)
    (d_x_norm,) = norm_attn_pull(seq_scatter(dh_attn_part))
    dx_in = (d_mid.astype(jnp.float32) + d_x_norm).astype(jnp.bfloat16)
    return y_out, dx_in, dw_qkv, dw_out, dw_gate, dw_up, dw_down


def solution(mesh):
    act_spec = P(FSDP_AXES, 'model', None)
    col_spec = P(FSDP_AXES, 'model')
    row_spec = P('model', FSDP_AXES)
    vec_spec = P(None)
    table_spec = P(None, None)
    in_specs = (act_spec, act_spec, vec_spec, vec_spec, col_spec, row_spec, col_spec, col_spec, row_spec, table_spec, table_spec)
    out_specs = (act_spec, act_spec, col_spec, row_spec, col_spec, col_spec, row_spec)
    return jax.shard_map(layer_body, mesh=mesh, in_specs=in_specs, out_specs=out_specs, check_vma=False)
```

profile of v0, /device:TPU:0, one launch (start us, length us, event | category | flops | bytes accessed | tf_op | source)
XLA Modules:
  0.0 2503.5 jit_solution(309944011036311003)
XLA Ops:
  24.2 52.7 %all-gather.12.cloned.1.call-done = bf16[2048,1536]{1,0:T(8,128)(2,1)} async-done(((bf16[512,1536]{1,0:T(8,128)(2,1)}), bf16[2048,1536]{1,0:T(8,128)(2,1)}) %all-gather.12.cloned.1.call-update) | async-done | bytes 6291472 | tf_op jit(solution)/shard_map/all_gather | solution.py:39
  76.9 29.9 %all-gather.10.cloned.1.call-done = bf16[32,128,2048]{2,1,0:T(8,128)(2,1)} async-done(((bf16[32,64,2048]{2,1,0:T(8,128)(2,1)}), bf16[32,128,2048]{2,1,0:T(8,128)(2,1)}) %all-gather.10.cloned.1.call-update) | async-done | bytes 16777232 | tf_op jit(solution)/shard_map/all_gather | solution.py:47
  106.9 33.7 %fusion.42 = f32[32,128,1536]{1,2,0:T(8,128)} fusion(bf16[32,128,2048]{2,1,0:T(8,128)(2,1)} %all-gather.10.cloned.1.call-done, bf16[2048,1536]{1,0:T(8,128)(2,1)} %all-gather.12.cloned.1.call-done), kind=kOutput, calls=%fused_computation.83 | convolution fusion | flops 25769803776 | bytes 48234496 | tf_op jit(solution)/shard_map/bsd,dc->bsc/dot_general | solution.py:67
  170.8 26.8 %fusion.13 = f32[32,4,4,128]{3,2,1,0:T(4,128)S(1)} fusion(f32[32,4,128,128,4]{3,2,4,1,0:T(8,128)} %get-tuple-element.19, f32[32,4,4,128]{3,2,1,0:T(4,128)S(1)} %get-tuple-element.18, pred[128,128]{0,1:T(8,128)(4,1)S(1)} %iota_compare_fusion.1), kind=kLoop, calls=%fused_computation.38 | loop fusion | flops 33488896 | bytes 34095104 | tf_op jit(solution)/shard_map/jvp()/reduce_sum | solution.py:33
  222.5 24.6 convolution_convert_fusion.2
  249.1 21.2 reduce-scatter.10.cloned.1.call-done
  300.6 154.5 %all-gather.22.cloned.1.call-done = bf16[4096,2048]{1,0:T(8,128)(2,1)} async-done(((bf16[4096,512]{1,0:T(8,128)(2,1)}), bf16[4096,2048]{1,0:T(8,128)(2,1)}) %all-gather.22.cloned.1.call-update) | async-done | bytes 16777232 | tf_op jit(solution)/shard_map/all_gather | solution.py:43
  455.1 77.8 %convolution_convert_fusion = bf16[32,128,4096]{2,1,0:T(8,128)(2,1)} fusion(bf16[32,128,2048]{2,1,0:T(8,128)(2,1)} %all-gather.24.cloned.1.call-done, bf16[4096,2048]{1,0:T(8,128)(2,1)} %all-gather.22.cloned.1.call-done), kind=kOutput, calls=%fused_computation.33 | convolution fusion | flops 68736253952 | bytes 67108864 | tf_op jit(solution)/shard_map/bsd,fd->bsf/dot_general | solution.py:92
  532.9 75.8 %all-gather.18.cloned.1.call-done = bf16[2048,4096]{1,0:T(8,128)(2,1)} async-done(((bf16[512,4096]{1,0:T(8,128)(2,1)}), bf16[2048,4096]{1,0:T(8,128)(2,1)}) %all-gather.18.cloned.1.call-update) | async-done | bytes 16777232 | tf_op jit(solution)/shard_map/all_gather | solution.py:39
  608.8 29.9 %all-gather.16.cloned.1.call-done = bf16[32,128,2048]{2,1,0:T(8,128)(2,1)} async-done(((bf16[32,64,2048]{2,1,0:T(8,128)(2,1)}), bf16[32,128,2048]{2,1,0:T(8,128)(2,1)}) %all-gather.16.cloned.1.call-update) | async-done | bytes 16777232 | tf_op jit(solution)/shard_map/all_gather | solution.py:47
  638.7 78.8 %fusion.36 = f32[32,128,4096]{2,1,0:T(8,128)} fusion(bf16[32,128,2048]{2,1,0:T(8,128)(2,1)} %all-gather.16.cloned.1.call-done, bf16[2048,4096]{1,0:T(8,128)(2,1)} %all-gather.18.cloned.1.call-done), kind=kOutput, calls=%fused_computation.64 | convolution fusion | flops 68719476736 | bytes 100663296 | tf_op jit(solution)/shard_map/bsd,df->bsf/dot_general | solution.py:81
  717.5 76.0 %all-gather.20.cloned.1.call-done = bf16[2048,4096]{1,0:T(8,128)(2,1)} async-done(((bf16[512,4096]{1,0:T(8,128)(2,1)}), bf16[2048,4096]{1,0:T(8,128)(2,1)}) %all-gather.20.cloned.1.call-update) | async-done | bytes 16777232 | tf_op jit(solution)/shard_map/all_gather | solution.py:39
  793.5 115.6 %fusion.2 = (bf16[32,128,4096]{2,1,0:T(8,128)(2,1)}, bf16[32,128,4096]{2,1,0:T(8,128)(2,1)}, bf16[32,128,4096]{2,1,0:T(8,128)(2,1)}) fusion(bf16[32,128,4096]{2,1,0:T(8,128)(2,1)} %convolution_convert_fusion, f32[32,128,4096]{2,1,0:T(8,128)} %fusion.36, bf16[32,128,2048]{2,1,0:T(8,128)(2,1)} %all-gather.16.cloned.1.call-done, ...), kind=kOutput, calls=%fused_computation.4 | convolution fusion | flops 68987912192 | bytes 234881024 | tf_op jit(solution)/shard_map/bsd,df->bsf/dot_general | solution.py:82
  909.1 78.8 %fusion.34 = f32[32,128,2048]{2,1,0:T(8,128)} fusion(bf16[32,128,4096]{2,1,0:T(8,128)(2,1)} %get-tuple-element.9, bf16[2048,4096]{1,0:T(8,128)(2,1)} %all-gather.18.cloned.1.call-done), kind=kOutput, calls=%fused_computation.62 | convolution fusion | flops 68719476736 | bytes 83886080 | tf_op jit(solution)/shard_map/bsf,df->bsd/dot_general | solution.py:100
  988.0 81.4 %add_convert_fusion = bf16[32,128,2048]{2,1,0:T(8,128)(2,1)} fusion(f32[32,128,2048]{2,1,0:T(8,128)} %fusion.34, bf16[32,128,4096]{2,1,0:T(8,128)(2,1)} %get-tuple-element.11, bf16[2048,4096]{1,0:T(8,128)(2,1)} %all-gather.20.cloned.1.call-done), kind=kOutput, calls=%fused_computation.19 | convolution fusion | flops 68736253952 | bytes 100663296 | tf_op jit(solution)/shard_map/bsf,df->bsd/dot_general | solution.py:101
  1069.5 77.9 %fusion.38 = bf16[32,128,2048]{2,1,0:T(8,128)(2,1)} fusion(bf16[32,128,4096]{2,1,0:T(8,128)(2,1)} %get-tuple-element.10, bf16[4096,2048]{1,0:T(8,128)(2,1)} %all-gather.22.cloned.1.call-done), kind=kOutput, calls=%fused_computation.68 | convolution fusion | flops 68727865344 | bytes 67108864 | tf_op jit(solution)/shard_map/bsf,fd->bsd/dot_general | solution.py:87
  1169.4 20.2 fusion.15
  1189.8 28.9 %all-gather.26.cloned.1.call-done = bf16[32,128,2048]{2,1,0:T(8,128)(2,1)} async-done(((bf16[32,64,2048]{2,1,0:T(8,128)(2,1)}), bf16[32,128,2048]{2,1,0:T(8,128)(2,1)}) %all-gather.26.cloned.1.call-update) | async-done | bytes 16777232 | tf_op jit(solution)/shard_map/all_gather | solution.py:47
  1218.7 24.3 convolution_convert_fusion.4
  1267.8 23.9 fusion.11
  1291.8 23.2 fusion.50
  1315.0 23.4 convert_bitcast_fusion.1
  1379.2 31.9 %convolution_convert_fusion.1 = bf16[32,128,2048]{2,1,0:T(8,128)(2,1)} fusion(bf16[32,128,1536]{1,2,0:T(8,128)(2,1)S(1)} %bitcast.146, bf16[2048,1536]{1,0:T(8,128)(2,1)} %all-gather.12.cloned.1.call-done), kind=kOutput, calls=%fused_computation.69 | convolution fusion | flops 25778192384 | bytes 35651584 | tf_op jit(solution)/shard_map/bsc,dc->bsd/dot_general | solution.py:118
  1411.2 24.0 convolution_bitcast_fusion.4
  1435.3 79.8 %convolution_bitcast_fusion.2 = f32[2048,4096]{1,0:T(8,128)} fusion(bf16[32,128,2048]{2,1,0:T(8,128)(2,1)} %all-gather.16.cloned.1.call-done, bf16[32,128,4096]{2,1,0:T(8,128)(2,1)} %get-tuple-element.9), kind=kOutput, calls=%fused_computation.41 | convolution fusion | flops 68719476736 | bytes 83886080 | tf_op jit(solution)/shard_map/bsd,bsf->df/dot_general | solution.py:102
  1515.2 79.6 %convolution_bitcast_fusion.1 = f32[2048,4096]{1,0:T(8,128)} fusion(bf16[32,128,2048]{2,1,0:T(8,128)(2,1)} %all-gather.16.cloned.1.call-done, bf16[32,128,4096]{2,1,0:T(8,128)(2,1)} %get-tuple-element.11), kind=kOutput, calls=%fused_computation.40 | convolution fusion | flops 68719476736 | bytes 83886080 | tf_op jit(solution)/shard_map/bsd,bsf->df/dot_general | solution.py:104
  1594.9 79.7 %convolution_bitcast_fusion = f32[4096,2048]{1,0:T(8,128)} fusion(bf16[32,128,4096]{2,1,0:T(8,128)(2,1)} %get-tuple-element.10, bf16[32,128,2048]{2,1,0:T(8,128)(2,1)} %all-gather.24.cloned.1.call-done), kind=kOutput, calls=%fused_computation.39 | convolution fusion | flops 68719476736 | bytes 83886080 | tf_op jit(solution)/shard_map/bsf,bsd->fd/dot_general | solution.py:94
  1674.7 34.7 %convolution_bitcast_fusion.3 = f32[2048,1536]{1,0:T(8,128)} fusion(bf16[32,128,2048]{2,1,0:T(8,128)(2,1)} %all-gather.10.cloned.1.call-done, bf16[32,128,1536]{1,2,0:T(8,128)(2,1)} %bitcast.147), kind=kOutput, calls=%fused_computation.77 | convolution fusion | flops 25769803776 | bytes 41943040 | tf_op jit(solution)/shard_map/bsd,bsc->dc/dot_general | solution.py:119
  1731.2 74.4 %reduce-scatter.22.cloned.1.call-done = f32[512,4096]{1,0:T(8,128)} async-done(((f32[2048,4096]{1,0:T(8,128)}), f32[512,4096]{1,0:T(8,128)}) %reduce-scatter.22.cloned.1.call-update) | async-done | bytes 8388624 | tf_op jit(solution)/shard_map/reduce_scatter | solution.py:102
  1805.6 286.2 %reduce-scatter.24.cloned.1.call-done = f32[512,4096]{1,0:T(8,128)} async-done(((f32[2048,4096]{1,0:T(8,128)}), f32[512,4096]{1,0:T(8,128)}) %reduce-scatter.24.cloned.1.call-update) | async-done | bytes 8388624 | tf_op jit(solution)/shard_map/reduce_scatter | solution.py:104
  2091.8 286.2 %reduce-scatter.26.cloned.1.call-done = f32[4096,512]{1,0:T(8,128)} async-done(((f32[4096,2048]{1,0:T(8,128)}), f32[4096,512]{1,0:T(8,128)}) %reduce-scatter.26.cloned.1.call-update) | async-done | bytes 8388624 | tf_op jit(solution)/shard_map/reduce_scatter | solution.py:94
  2378.1 118.3 %reduce-scatter.18.cloned.1.call-done = f32[512,1536]{1,0:T(8,128)} async-done(((f32[2048,1536]{1,0:T(8,128)}), f32[512,1536]{1,0:T(8,128)}) %reduce-scatter.18.cloned.1.call-update) | async-done | bytes 3145744 | tf_op jit(solution)/shard_map/reduce_scatter | solution.py:119
  (113 shorter events, 214.0 us)
Async XLA Ops:
  7.2 69.8 %all-gather.12.cloned.1.call-start = ((), (), s32[]{:S(2)}) async-start(), calls=%async_computation.10 | async-start | bytes 7864320 | tf_op jit(solution)/shard_map/all_gather | solution.py:39
  7.9 99.0 %all-gather.10.cloned.1.call-start = ((), (), s32[]{:S(2)}) async-start(), calls=%async_computation.9 | async-start | bytes 25165824 | tf_op jit(solution)/shard_map/all_gather | solution.py:47
  23.0 199.5 %all-gather.14.cloned.1.call-start = ((), (), s32[]{:S(2)}) async-start(), calls=%async_computation.11 | async-start | bytes 5242880 | tf_op jit(solution)/shard_map/all_gather | solution.py:43
  23.7 246.5 %reduce-scatter.10.cloned.1.call-start = ((), (), s32[]{:S(2)}) async-start(), calls=%async_computation.12 | async-start | bytes 25165824 | tf_op jit(solution)/shard_map/reduce_scatter | solution.py:51
  24.2 173.4 %copy-start.8 = (pred[128,128]{0,1:T(8,128)(4,1)}, pred[128,128]{0,1:T(8,128)(4,1)S(1)}, u32[]{:S(2)}) copy-start(pred[128,128]{0,1:T(8,128)(4,1)S(1)} %iota_compare_fusion.1) | copy-start | bytes 49156
  24.2 116.4 %copy-start.19 = (f32[128,32]{0,1:T(8,128)S(1)}, f32[128,32]{0,1:T(8,128)}, u32[]{:S(2)}) copy-start(f32[128,32]{0,1:T(8,128)} %param.21) | copy-start | bytes 49156
  24.2 116.4 %copy-start.21 = (f32[128,32]{0,1:T(8,128)S(1)}, f32[128,32]{0,1:T(8,128)}, u32[]{:S(2)}) copy-start(f32[128,32]{0,1:T(8,128)} %param.20) | copy-start | bytes 49156
  170.8 26.8 %copy-start.4 = (f32[32,4,4,128]{3,2,1,0:T(4,128)}, f32[32,4,4,128]{3,2,1,0:T(4,128)S(1)}, u32[]{:S(2)}) copy-start(f32[32,4,4,128]{3,2,1,0:T(4,128)S(1)} %get-tuple-element.18) | copy-start | bytes 786436
  170.8 27.5 %copy-start = (f32[32,4,128,128,4]{3,2,4,1,0:T(8,128)S(1)}, f32[32,4,128,128,4]{3,2,4,1,0:T(8,128)}, u32[]{:S(2)}) copy-start(f32[32,4,128,128,4]{3,2,4,1,0:T(8,128)} %get-tuple-element.19) | copy-start | bytes 100663296
  247.1 53.5 %all-gather.24.cloned.1.call-start = ((), (), s32[]{:S(2)}) async-start(), calls=%async_computation.18 | async-start | bytes 25165824 | tf_op jit(solution)/shard_map/all_gather | solution.py:47
  247.7 34.3 %copy-start.16 = (f32[2048]{0:T(1024)S(1)}, f32[2048]{0:T(1024)}, u32[]{:S(2)}) copy-start(f32[2048]{0:T(1024)} %param.14) | copy-start | bytes 24580
  247.7 207.4 %all-gather.22.cloned.1.call-start = ((), (), s32[]{:S(2)}) async-start(), calls=%async_computation.16 | async-start | bytes 20971520 | tf_op jit(solution)/shard_map/all_gather | solution.py:43
  248.3 360.5 %all-gather.18.cloned.1.call-start = ((), (), s32[]{:S(2)}) async-start(), calls=%async_computation.14 | async-start | bytes 20971520 | tf_op jit(solution)/shard_map/all_gather | solution.py:39
  249.0 389.7 %all-gather.16.cloned.1.call-start = ((), (), s32[]{:S(2)}) async-start(), calls=%async_computation.13 | async-start | bytes 25165824 | tf_op jit(solution)/shard_map/all_gather | solution.py:47
  290.8 502.8 %all-gather.20.cloned.1.call-start = ((), (), s32[]{:S(2)}) async-start(), calls=%async_computation.15 | async-start | bytes 20971520 | tf_op jit(solution)/shard_map/all_gather | solution.py:39
  291.5 856.0 %reduce-scatter.14.cloned.1.call-start = ((), (), s32[]{:S(2)}) async-start(), calls=%async_computation.19 | async-start | bytes 25165824 | tf_op jit(solution)/shard_map/reduce_scatter | solution.py:51
  1069.4 100.0 %reduce-scatter.12.cloned.1.call-start = ((), (), s32[]{:S(2)}) async-start(), calls=%async_computation.17 | async-start | bytes 25165824 | tf_op jit(solution)/shard_map/reduce_scatter | solution.py:51
  1147.4 9.2 copy-start.15
  1147.4 22.0 copy-start.11
  1147.4 71.3 %all-gather.26.cloned.1.call-start = ((), (), s32[]{:S(2)}) async-start(), calls=%async_computation.20 | async-start | bytes 25165824 | tf_op jit(solution)/shard_map/all_gather | solution.py:47
  1156.6 33.0 %copy-start.3 = (f32[32,4,4,128]{3,2,1,0:T(4,128)S(1)}, f32[32,4,4,128]{3,2,1,0:T(4,128)}, u32[]{:S(2)}) copy-start(f32[32,4,4,128]{3,2,1,0:T(4,128)} %copy-done.2) | copy-start | bytes 786436
  1189.6 519.9 %reduce-scatter.16.cloned.1.call-start = ((), (), s32[]{:S(2)}) async-start(), calls=%async_computation.21 | async-start | bytes 25165824 | tf_op jit(solution)/shard_map/reduce_scatter | solution.py:51
  1254.9 12.9 copy-start.5
  1254.9 12.9 copy-start.9
  1338.5 11.8 copy-start.20
  1338.5 11.8 copy-start.22
  1411.1 320.1 %reduce-scatter.20.cloned.1.call-start = ((), (), s32[]{:S(2)}) async-start(), calls=%async_computation.23 | async-start | bytes 10485760 | tf_op jit(solution)/shard_map/reduce_scatter | solution.py:112
  1435.2 370.4 %reduce-scatter.22.cloned.1.call-start = ((), (), s32[]{:S(2)}) async-start(), calls=%async_computation.24 | async-start | bytes 41943040 | tf_op jit(solution)/shard_map/reduce_scatter | solution.py:102
  1515.1 576.7 %reduce-scatter.24.cloned.1.call-start = ((), (), s32[]{:S(2)}) async-start(), calls=%async_computation.25 | async-start | bytes 41943040 | tf_op jit(solution)/shard_map/reduce_scatter | solution.py:104
  1594.8 783.3 %reduce-scatter.26.cloned.1.call-start = ((), (), s32[]{:S(2)}) async-start(), calls=%async_computation.26 | async-start | bytes 41943040 | tf_op jit(solution)/shard_map/reduce_scatter | solution.py:94
  1674.6 34.9 %copy-start.18 = (f32[2048]{0:T(1024)S(1)}, f32[2048]{0:T(1024)}, u32[]{:S(2)}) copy-start(f32[2048]{0:T(1024)} %param.13) | copy-start | bytes 24580
  1674.6 821.8 %reduce-scatter.18.cloned.1.call-start = ((), (), s32[]{:S(2)}) async-start(), calls=%async_computation.22 | async-start | bytes 15728640 | tf_op jit(solution)/shard_map/reduce_scatter | solution.py:119
  (9 other events, 25.6 us)
Sparse Core Ops, SparseCore 0:
  9.7 67.1 all-gather.11
  79.0 27.8 all-gather.9
  108.6 47.6 all-gather.13
  247.2 22.9 reduce-scatter.9
  271.6 28.9 all-gather.23
  302.2 152.8 all-gather.21
  456.9 151.8 all-gather.17
  610.9 27.8 all-gather.15
  640.5 153.0 all-gather.19
  1069.6 21.7 reduce-scatter.13
  1147.5 21.7 reduce-scatter.11
  1189.7 28.9 all-gather.25
  1411.2 22.9 reduce-scatter.15
  1437.7 81.6 reduce-scatter.19
  1522.8 282.7 reduce-scatter.21
  1809.0 282.7 reduce-scatter.23
  2095.3 282.7 reduce-scatter.25
  2381.5 114.8 reduce-scatter.17
where the time goes:
time: 2500 us
  waiting for transfers between devices  1260 us (50%)
  matrix products  1040 us (42%)
  other arithmetic  171 us (7%)
    reduce_scatter x1, waiting for transfers between devices, layer_body(): lax.psum_scatter(jnp.einsum('bsd,bsf->df', h_mlp_full, d_up, preferred_el...  286 us
    reduce_scatter x1, waiting for transfers between devices, layer_body(): lax.psum_scatter(jnp.einsum('bsf,bsd->fd', act_val, grad_full, preferred_...  286 us
    all_gather x3, waiting for transfers between devices, gather_rows(): return lax.all_gather(w_shard, FSDP_AXES, axis=0, tiled=True)  205 us
    all_gather x2, waiting for transfers between devices, gather_cols(): return lax.all_gather(w_shard, FSDP_AXES, axis=1, tiled=True)  155 us
    reduce_scatter x1, waiting for transfers between devices, layer_body(): lax.psum_scatter(jnp.einsum('bsd,bsc->dc', h_attn_full, d_qkv, preferred_...  118 us
    dot_general x1, matrix products, layer_body(): jnp.einsum('bsd,df->bsf', h_mlp_full, up_full, preferred_element_type=jnp...  116 us
    all_gather x4, waiting for transfers between devices, seq_gather(): return lax.all_gather(act_shard, 'model', axis=1, tiled=True)  97.9 us
    dot_general x1, matrix products, layer_body(): jnp.einsum('bsf,df->bsd', d_up, up_again, preferred_element_type=jnp.floa...  81.4 us
  transfers between devices with their start and end apart: 18, of which 14 were waited for; matrix products, arithmetic and copies ran while one was open for 28% of the time, Pallas kernels for 0%

commit v1 on v0

v1 whole, which is shorter than its diff:
```python
import functools
import jax
import jax.numpy as jnp
from jax import lax
from jax.experimental import pallas as pl
from jax.experimental.pallas import tpu as pltpu
from jax.sharding import PartitionSpec as P

FSDP_AXES = ('data', 'fsdp')
SWAP = ((0, 1), (1, 0))
F32 = jnp.float32
BF16 = jnp.bfloat16
NN = (((1,), (0,)), ((), ()))
NT = (((1,), (1,)), ((), ()))
TN = (((0,), (0,)), ((), ()))
ANY = pl.BlockSpec(memory_space=pl.ANY)
EPS = 1e-5
HEAD = 64


def dot(a, b, dims=NN):
    return lax.dot_general(a, b, dims, preferred_element_type=F32)


def params(mib=60):
    return pltpu.CompilerParams(vmem_limit_bytes=mib * 1024 * 1024)


def cost(flops, nbytes, trans=0):
    return pl.CostEstimate(flops=int(flops), bytes_accessed=int(nbytes), transcendentals=int(trans))


def scalar_call(body, grid, in_specs, out_specs, out_shape, scratch=(), alias=None, ce=None):
    return pl.pallas_call(
        body, out_shape=out_shape,
        grid_spec=pltpu.PrefetchScalarGridSpec(num_scalar_prefetch=1, grid=grid, in_specs=in_specs, out_specs=out_specs,
                                               scratch_shapes=list(scratch)),
        input_output_aliases=alias or {}, compiler_params=params(), cost_estimate=ce)


class Weight:
    def __init__(self, shape, axis, pieces):
        self.shape, self.axis, self.pieces = shape, axis, pieces

    def arrays(self):
        return [p[0] for p in self.pieces]

    def copies(self, ids, refs, dst, sem, base):
        blk = self.shape[self.axis] // 4
        out = []
        for i, (ref, (arr, j, off)) in enumerate(zip(refs, self.pieces)):
            n = arr.shape[1 - self.axis]
            at = [pl.ds(off, n), pl.ds(off, n)]
            at[self.axis] = pl.ds(pl.multiple_of(ids[j] * blk, blk), blk)
            out.append(pltpu.make_async_copy(ref, dst.at[at[0], at[1]], sem.at[base + i]))
        return out


def load_all(ids, weights, refs, dsts, sem):
    copies, n = [], 0
    for w, dst in zip(weights, dsts):
        copies += w.copies(ids, refs[n:n + len(w.pieces)], dst, sem, n)
        n += len(w.pieces)
    for c in copies:
        c.start()
    for c in copies:
        c.wait()


def weight_scratch(weights):
    return [pltpu.VMEM(w.shape, BF16) for w in weights] + [pltpu.SemaphoreType.DMA((sum(len(w.pieces) for w in weights),))]


def rms_f(v, gain):
    return (v * lax.rsqrt(jnp.mean(v * v, axis=-1, keepdims=True) + EPS) * gain).astype(BF16)


def rms_b(v, gain, dh):
    r = lax.rsqrt(jnp.mean(v * v, axis=-1, keepdims=True) + EPS)
    gd = gain * dh
    return r * gd - v * (r * r * r * jnp.mean(v * gd, axis=-1, keepdims=True))


def rms_kernel(x_ref, gain_ref, h_ref):
    h_ref[...] = rms_f(x_ref[...].astype(F32), gain_ref[...])


def rms_call(x, gain, tile=256):
    t, d = x.shape
    row = pl.BlockSpec((tile, d), lambda i: (i, 0))
    return pl.pallas_call(rms_kernel, grid=(t // tile,), in_specs=[row, pl.BlockSpec((1, d), lambda i: (0, 0))],
                          out_specs=row, out_shape=jax.ShapeDtypeStruct((t, d), BF16), compiler_params=params(),
                          cost_estimate=cost(t * d * 8, 4 * t * d))(x, gain)


def rope(x, c, s, sign):
    lane = lax.broadcasted_iota(jnp.int32, x.shape, x.ndim - 1)
    partner = jnp.where(lane % HEAD < HEAD // 2, pltpu.roll(x, 96, x.ndim - 1), pltpu.roll(x, 32, x.ndim - 1))
    return x * c + (partner * s if sign > 0 else -(partner * s))


def qkv_kernel(w, seq_loc, ids, h_ref, c_ref, s_ref, *refs):
    n = len(w.pieces)
    out, wv, sem = refs[n:]

    @pl.when(pl.program_id(0) == 0)
    def _():
        load_all(ids, [w], refs[:n], [wv], sem)

    h = h_ref[...]
    nb = h.shape[0] // seq_loc
    for g in range(w.shape[1] // 768):
        acc = dot(h, wv[:, g * 768:(g + 1) * 768])
        for q in range(6):
            k = q % 3
            part = acc[:, q * 128:(q + 1) * 128].reshape(nb, seq_loc, 128)
            cs = c_ref[0, :, k * 128:(k + 1) * 128][None]
            sn = s_ref[0, :, k * 128:(k + 1) * 128][None]
            lo = g * 768 + q * 128
            out[:, lo:lo + 128] = rope(part, cs, sn, 1).astype(BF16).reshape(nb * seq_loc, 128)


def qkv_call(ids, h, w, cos_t, sin_t, tile=512):
    t, d = h.shape
    width = w.shape[1]
    seq_loc = cos_t.shape[1]
    nt = t // tile
    tab = pl.BlockSpec((1, seq_loc, 384), lambda i, s: (i * 2 // nt, 0, 0))
    return scalar_call(functools.partial(qkv_kernel, w, seq_loc), (nt,),
                       [pl.BlockSpec((tile, d), lambda i, s: (i, 0)), tab, tab] + [ANY] * len(w.pieces),
                       pl.BlockSpec((tile, width), lambda i, s: (i, 0)), jax.ShapeDtypeStruct((t, width), BF16),
                       weight_scratch([w]), ce=cost(2 * t * d * width, 2 * (t * d + d * width + t * width)))(
        ids, h, cos_t, sin_t, *w.arrays())


def spread(kv):
    f = kv.astype(F32)
    lane = lax.broadcasted_iota(jnp.int32, f.shape, 1)
    k0 = jnp.where(lane < HEAD, f, 0.0)
    v1 = jnp.where(lane < HEAD, 0.0, f)
    kz = jnp.concatenate([k0, pltpu.roll(k0, HEAD, 1)], axis=0).astype(BF16)
    vz = jnp.concatenate([pltpu.roll(v1, HEAD, 1), v1], axis=0).astype(BF16)
    return kz, vz


def probs(q, kz, seq):
    s = dot(kz, q, NT) * (HEAD ** -0.5)
    t = lax.broadcasted_iota(jnp.int32, (seq, 2 * seq), 0)
    pos = lax.broadcasted_iota(jnp.int32, (seq, 2 * seq), 1) % seq
    out = []
    for h in range(2):
        sh = jnp.where(pos >= t, s[h * seq:(h + 1) * seq], -1e30)
        e = jnp.exp(sh - jnp.max(sh, axis=0, keepdims=True))
        out.append(e * (1.0 / jnp.sum(e, axis=0, keepdims=True)))
    return out


def pair_rows(ref, b, seq, first):
    lo = ref[:, b, :, first:first + 128].reshape(seq, 128)
    hi = ref[:, b, :, first + 128:first + 256].reshape(seq, 128)
    return jnp.concatenate([lo, hi], axis=0)


def attn_kernel(nb, seq, qkv_ref, o_ref):
    half = seq // 2
    for b in range(nb):
        q = pair_rows(qkv_ref, b, seq, 0)
        kz, vz = spread(qkv_ref[:, b, :, 256:384].reshape(seq, 128))
        p = jnp.concatenate(probs(q, kz, seq), axis=0).astype(BF16)
        o = dot(p, vz, TN).astype(BF16)
        o_ref[:, b, :, 0:128] = o[:seq].reshape(2, half, 128)
        o_ref[:, b, :, 128:256] = o[seq:].reshape(2, half, 128)


def attn_call(qkv, nb=16):
    two, batch, half, width = qkv.shape
    groups = width // 384
    seq = two * half
    spec = lambda n: pl.BlockSpec((2, nb, half, n), lambda i, j: (0, i, 0, j))
    return pl.pallas_call(functools.partial(attn_kernel, nb, seq), grid=(batch // nb, groups), in_specs=[spec(384)],
                          out_specs=spec(256), out_shape=jax.ShapeDtypeStruct((2, batch, half, groups * 256), BF16),
                          compiler_params=params(), cost_estimate=cost(8e9, 20e6, 4e6))(qkv)


def attn_bwd_kernel(nb, seq, qkv_ref, do_ref, c_ref, s_ref, out_ref):
    half = seq // 2
    cos_t = [c_ref[:, :, k * 128:(k + 1) * 128].reshape(seq, 128) for k in range(3)]
    sin_t = [s_ref[:, :, k * 128:(k + 1) * 128].reshape(seq, 128) for k in range(3)]
    for b in range(nb):
        q = pair_rows(qkv_ref, b, seq, 0)
        do = pair_rows(do_ref, b, seq, 0)
        kz, vz = spread(qkv_ref[:, b, :, 256:384].reshape(seq, 128))
        ps = probs(q, kz, seq)
        dp = dot(vz, do, NT)
        ds = []
        for h in range(2):
            d = dp[h * seq:(h + 1) * seq].astype(BF16).astype(F32)
            ds.append(ps[h] * (d - jnp.sum(ps[h] * d, axis=0, keepdims=True)) * (HEAD ** -0.5))
        ds = jnp.concatenate(ds, axis=0).astype(BF16)
        p = jnp.concatenate(ps, axis=0).astype(BF16)
        dq = dot(ds, kz, TN).astype(BF16).astype(F32)
        rk = dot(ds, q)
        rv = dot(p, do)
        lane = lax.broadcasted_iota(jnp.int32, (seq, 128), 1)
        dkv = jnp.where(lane < HEAD, rk[:seq] + pltpu.roll(rk[seq:], HEAD, 1), pltpu.roll(rv[:seq], HEAD, 1) + rv[seq:])
        dkv = dkv.astype(BF16).astype(F32)
        for k, part in enumerate((dq[:seq], dq[seq:], dkv)):
            out_ref[:, b, :, k * 128:(k + 1) * 128] = rope(part, cos_t[k], sin_t[k], -1).astype(BF16).reshape(2, half, 128)


def attn_bwd_call(qkv, d_o, cos_t, sin_t, nb=8):
    two, batch, half, width = qkv.shape
    groups = width // 384
    seq = two * half
    spec = lambda n: pl.BlockSpec((2, nb, half, n), lambda i, j: (0, i, 0, j))
    tab = pl.BlockSpec((2, half, 384), lambda i, j: (0, 0, 0))
    return pl.pallas_call(functools.partial(attn_bwd_kernel, nb, seq), grid=(batch // nb, groups),
                          in_specs=[spec(384), spec(256), tab, tab], out_specs=spec(384),
                          out_shape=jax.ShapeDtypeStruct(qkv.shape, BF16), compiler_params=params(),
                          cost_estimate=cost(20e9, 40e6, 8e6))(qkv, d_o, cos_t, sin_t)


def mlp_kernel(ws, nc, ids, h_ref, g_ref, *refs):
    n = sum(len(w.pieces) for w in ws)
    act_ref, dgu_ref, wgu, wd, sem = refs[n:]

    @pl.when(pl.program_id(0) == 0)
    def _():
        load_all(ids, ws, refs[:n], [wgu, wd], sem)

    width = wd.shape[0]
    step = width // nc
    h = h_ref[...]
    g = g_ref[...]
    for c in range(nc):
        cols, ucols = pl.ds(c * step, step), pl.ds(width + c * step, step)
        gate = dot(h, wgu[:, cols])
        up = dot(h, wgu[:, ucols])
        d_act = dot(g, wd[cols, :], NT).astype(BF16).astype(F32)
        sig = jax.nn.sigmoid(gate)
        gate_act = gate * sig
        act_ref[:, cols] = (gate_act * up).astype(BF16)
        dgu_ref[:, ucols] = (d_act * gate_act).astype(BF16)
        dgu_ref[:, cols] = (d_act * up * sig * (1.0 + gate * (1.0 - sig))).astype(BF16)


def mlp_call(ids, h, g, wgu, wd, tile=512, nc=8):
    t, d = h.shape
    f = wd.shape[0]
    row = lambda n: pl.BlockSpec((tile, n), lambda i, s: (i, 0))
    ws = [wgu, wd]
    arrs = wgu.arrays() + wd.arrays()
    return scalar_call(functools.partial(mlp_kernel, ws, nc), (t // tile,), [row(d), row(d)] + [ANY] * len(arrs),
                       [row(f), row(2 * f)], [jax.ShapeDtypeStruct((t, f), BF16), jax.ShapeDtypeStruct((t, 2 * f), BF16)],
                       weight_scratch(ws), ce=cost(6 * t * d * f, 4 * t * d + 6 * d * f + 6 * t * f, t * f))(ids, h, g, *arrs)


def proj_kernel(ws, dims, n_extra, epi, ids, *refs):
    k = len(ws)
    n = sum(len(w.pieces) for w in ws)
    lhs, extra, pieces = refs[:k], refs[k:k + n_extra], refs[k + n_extra:k + n_extra + n]
    outs, dsts, sem = refs[k + n_extra + n:-k - 1], refs[-k - 1:-1], refs[-1]
    first = pl.program_id(0) == 0

    def body(waits):
        acc = None
        for i in range(k):
            for c in waits[i]:
                c.wait()
            for lo in range(0, lhs[i].shape[1], 2048):
                part = pl.ds(lo, min(2048, lhs[i].shape[1]))
                d = dot(lhs[i][:, part], dsts[i][part, :] if dims is NN else dsts[i][:, part], dims)
                acc = d if acc is None else acc + d
        epi(acc, extra, outs)

    @pl.when(first)
    def _():
        groups, m = [], 0
        for w, dst in zip(ws, dsts):
            groups.append(w.copies(ids, pieces[m:m + len(w.pieces)], dst, sem, m))
            m += len(w.pieces)
        for c in sum(groups, []):
            c.start()
        body(groups)

    @pl.when(jnp.logical_not(first))
    def _():
        body([[]] * k)


def proj_call(ids, lhs, ws, dims, rows, which, epi, extra, outs, tile=256):
    t = rows
    kdim = lhs[0].shape[1]
    nout = ws[0].shape[1] if dims is NN else ws[0].shape[0]
    nt = t // tile
    if which is None:
        lrow = pl.BlockSpec((tile, kdim), lambda i, s: (i, 0))
    else:
        lrow = pl.BlockSpec((tile, kdim), lambda i, s: (s[which] * nt + i, 0))
    row = pl.BlockSpec((tile, nout), lambda i, s: (i, 0))
    espec = [row if e.shape[0] == t else pl.BlockSpec((1, nout), lambda i, s: (0, 0)) for e in extra]
    arrs = sum([w.arrays() for w in ws], [])
    return scalar_call(functools.partial(proj_kernel, ws, dims, len(extra), epi), (nt,),
                       [lrow] * len(lhs) + espec + [ANY] * len(arrs), [row] * outs,
                       [jax.ShapeDtypeStruct((t, nout), BF16)] * outs, weight_scratch(ws),
                       ce=cost(2 * t * kdim * nout * len(ws), 2 * len(ws) * (t * kdim + kdim * nout) + 2 * t * nout * (outs + len(extra))))(
        ids, *lhs, *extra, *arrs)


def epi_round(acc, extra, outs):
    outs[0][...] = acc.astype(BF16)


def epi_mid(acc, extra, outs):
    recv, x, gain = extra
    s = (acc + recv[...].astype(F32)).astype(BF16).astype(F32)
    mid = (x[...].astype(F32) + s).astype(BF16)
    outs[0][...] = mid
    outs[1][...] = rms_f(mid.astype(F32), gain[...])


def epi_add(acc, extra, outs):
    recv, mid = extra
    s = (acc + recv[...].astype(F32)).astype(BF16).astype(F32)
    outs[0][...] = (mid[...].astype(F32) + s).astype(BF16)


def epi_rms_b(acc, extra, outs):
    recv, v, res, gain = extra
    dh = (acc + recv[...].astype(F32)).astype(BF16).astype(F32)
    outs[0][...] = (res[...].astype(F32) + rms_b(v[...].astype(F32), gain[...], dh)).astype(BF16)


def tn_kernel(adds, ids, a_ref, b_ref, *refs):
    out = refs[-1]
    acc = dot(a_ref[...], b_ref[...], TN)
    for i in range(adds):
        acc += refs[i][...]
    out[...] = acc


def tn_call(ids, a, b, side, blocks, adds=(), into=None, out_shape=None, place=0):
    t = a.shape[0]
    dblk = 512
    nb = len(blocks)
    other = (b if side == 0 else a).shape[1]
    ot = (1024 if other % 1024 == 0 else 768) if side == 0 else 512
    no = other // ot

    def dsel(i, s):
        v = s[blocks[0]]
        for k in range(1, nb):
            v = jnp.where(i == k, s[blocks[k]], v)
        return v

    if side == 0:
        a_spec = pl.BlockSpec((t, dblk), lambda j, i, s: (0, dsel(i, s)))
        b_spec = pl.BlockSpec((t, ot), lambda j, i, s: (0, j))
        blk, add_map = (dblk, ot), lambda j, i, s: (i, j)
        shape, off = (nb * dblk, other), place // ot
        out_map = lambda j, i, s: (i, j + off)
    else:
        a_spec = pl.BlockSpec((t, ot), lambda j, i, s: (0, j))
        b_spec = pl.BlockSpec((t, dblk), lambda j, i, s: (0, dsel(i, s)))
        blk, add_map = (ot, dblk), lambda j, i, s: (j, i)
        shape, off = (other, nb * dblk), place // ot
        out_map = lambda j, i, s: (j + off, i)
    shape = out_shape or shape
    extra_in, extra_spec, alias = [], [], None
    if into is not None:
        extra_in, extra_spec, alias = [into], [ANY], {3 + len(adds): 0}
    return scalar_call(functools.partial(tn_kernel, len(adds)), (no, nb),
                       [a_spec, b_spec] + [pl.BlockSpec(blk, add_map)] * len(adds) + extra_spec, pl.BlockSpec(blk, out_map),
                       jax.ShapeDtypeStruct(shape, F32), alias=alias,
                       ce=cost(2 * t * nb * dblk * other, 2 * t * (nb * dblk + other) + 4 * nb * dblk * other * (1 + len(adds))))(
        ids, a, b, *adds, *extra_in)


def tn2_kernel(adds, half, ids, a_ref, b_ref, *refs):
    lo, hi = refs[-2:]
    acc = dot(a_ref[...], b_ref[...], TN)
    for i in range(adds):
        acc += refs[i][...]
    left = pl.program_id(0) < half

    @pl.when(left)
    def _():
        lo[...] = acc

    @pl.when(jnp.logical_not(left))
    def _():
        hi[...] = acc


def tn2_call(ids, a, b, adds, shape, place, into):
    t, dblk, ot = a.shape[0], 512, 1024
    n = b.shape[1] // ot
    half, off = n // 2, place // ot
    tile = pl.BlockSpec((dblk, ot), lambda j, s: (0, j))
    outs = [pl.BlockSpec((dblk, ot), lambda j, s: (0, jnp.minimum(j, half - 1) + off)),
            pl.BlockSpec((dblk, ot), lambda j, s: (0, jnp.maximum(j - half, 0) + off))]
    extra = list(into or ())
    return scalar_call(functools.partial(tn2_kernel, len(adds), half), (n,),
                       [pl.BlockSpec((t, dblk), lambda j, s: (0, s[0])), pl.BlockSpec((t, ot), lambda j, s: (0, j))]
                       + [tile] * len(adds) + [ANY] * len(extra), outs, [jax.ShapeDtypeStruct(shape, F32)] * 2,
                       alias={3 + len(adds) + k: k for k in range(len(extra))},
                       ce=cost(2 * t * dblk * b.shape[1], 2 * t * (dblk + b.shape[1]) + 12 * dblk * b.shape[1]))(
        ids, a, b, *adds, *extra)


def px(v):
    return lax.ppermute(v, 'fsdp', SWAP)


def py(v):
    return lax.ppermute(v, 'data', SWAP)


def pm(v):
    return lax.ppermute(v, 'model', SWAP)


def gather(axis, w):
    split = 1 - axis
    half = w.shape[split] // 2
    shape = list(w.shape)
    shape[axis] *= 4
    w_x = px(w)
    w_y = py(w)
    d_a = py(lax.slice_in_dim(w_x, 0, half, axis=split))
    d_b = px(lax.slice_in_dim(w_y, half, 2 * half, axis=split))
    return Weight(tuple(shape), axis, [(w, 0, 0), (w_x, 1, 0), (w_y, 2, 0), (d_a, 3, 0), (d_b, 3, half)])


def layer_impl(x_in, grad_out, gain_attn, gain_mlp, w_qkv, w_out, w_gate, w_up, w_down, rope_cos, rope_sin):
    batch, seq_loc, d_model = x_in.shape
    rows = batch * seq_loc
    width = w_qkv.shape[1]
    attn_w = w_out.shape[0]
    ffn = w_gate.shape[1]
    fh = ffn // 2
    me = lax.axis_index('data') * 2 + lax.axis_index('fsdp')
    core = lax.axis_index('model')
    ids = jnp.stack([me, me ^ 1, me ^ 2, me ^ 3, core, 1 - core]).astype(jnp.int32)
    own, oth = 4, 5

    x = x_in.reshape(rows, d_model)
    grad = grad_out.reshape(rows, d_model)
    g1, g2 = gain_attn.reshape(1, d_model), gain_mlp.reshape(1, d_model)
    one, zero = jnp.ones_like(rope_cos), jnp.zeros_like(rope_cos)
    cos_t = jnp.concatenate([rope_cos] * 10 + [one, one], axis=1).reshape(2, seq_loc, 6 * HEAD)
    sin_t = jnp.concatenate([-rope_sin, rope_sin] * 5 + [zero, zero], axis=1).reshape(2, seq_loc, 6 * HEAD)

    def both(v):
        return lax.all_gather(v, 'model', axis=0, tiled=True)

    def half_w(w, axis, i):
        return lax.slice_in_dim(w, i * fh, (i + 1) * fh, axis=axis)

    wq = gather(0, w_qkv)
    wo = gather(1, w_out)
    wgu, wd = [], []
    for i in range(2):
        wgu.append(gather(0, jnp.concatenate([half_w(w_gate, 1, i), half_w(w_up, 1, i)], axis=1)))
        wd.append(gather(1, half_w(w_down, 0, i)))

    h_s = rms_call(x, g1)
    h = both(h_s)
    g_full = both(grad)
    qkv = qkv_call(ids, h, wq, cos_t, sin_t).reshape(2, batch, seq_loc, width)
    o = attn_call(qkv).reshape(2 * rows, attn_w)
    part, = proj_call(ids, [o], [wo], NN, rows, oth, epi_round, [], 1)
    recv = pm(part)
    mid, h2_s = proj_call(ids, [o], [wo], NN, rows, own, epi_mid, [recv, x, g2], 2)
    h2 = both(h2_s)
    act, dgu = [None] * 2, [None] * 2
    for i in range(2):
        act[i], dgu[i] = mlp_call(ids, h2, g_full, wgu[i], wd[i])
    part, = proj_call(ids, act, wd, NN, rows, oth, epi_round, [], 1)
    recv = pm(part)
    y, = proj_call(ids, act, wd, NN, rows, own, epi_add, [recv, mid], 1)

    part, = proj_call(ids, dgu, wgu, NT, rows, oth, epi_round, [], 1)
    recv = pm(part)
    d_mid_s, = proj_call(ids, dgu, wgu, NT, rows, own, epi_rms_b, [recv, mid, grad, g2], 1)
    d_mid = both(d_mid_s)
    d_o, = proj_call(ids, [d_mid], [wo], NT, 2 * rows, None, epi_round, [], 1)
    d_qkv = attn_bwd_call(qkv, d_o.reshape(2, batch, seq_loc, attn_w), cos_t, sin_t).reshape(2 * rows, width)
    part, = proj_call(ids, [d_qkv], [wq], NT, rows, oth, epi_round, [], 1)
    recv = pm(part)
    dx, = proj_call(ids, [d_qkv], [wq], NT, rows, own, epi_rms_b, [recv, x, d_mid_s, g1], 1)

    def wsum(a, b, side, mode, last):
        first, second, j1, j2 = (px, py, 1, 2) if mode else (py, px, 2, 1)
        p3 = tn_call(ids, a, b, side, [3])
        r3 = first(p3)
        p1 = tn_call(ids, a, b, side, [j1])
        r1 = first(p1)
        p2 = tn_call(ids, a, b, side, [j2], [r3])
        r2 = second(p2)
        return last(r1, r2)

    dw_down = dw_gu = None
    for i in range(2):
        dw_down = wsum(act[i], g_full, 1, i == 0, lambda r1, r2: tn_call(
            ids, act[i], g_full, 1, [0], [r1, r2], dw_down, out_shape=(ffn, 512), place=i * fh))
        dw_gu = wsum(h2, dgu[i], 0, i == 1, lambda r1, r2: tn2_call(
            ids, h2, dgu[i], [r1, r2], (512, ffn), i * fh, dw_gu))
    dw_gate, dw_up = dw_gu
    dw_out = wsum(o, d_mid, 1, True, lambda r1, r2: tn_call(ids, o, d_mid, 1, [0]) + r1 + r2)
    dw_qkv = wsum(h, d_qkv, 0, False, lambda r1, r2: tn_call(ids, h, d_qkv, 0, [0]) + r1 + r2)
    return (y.reshape(x_in.shape), dx.reshape(x_in.shape), dw_qkv, dw_out, dw_gate, dw_up, dw_down)


def solution(mesh):
    act_spec = P(FSDP_AXES, 'model', None)
    col_spec = P(FSDP_AXES, 'model')
    row_spec = P('model', FSDP_AXES)
    vec_spec = P(None)
    table_spec = P(None, None)
    in_specs = (act_spec, act_spec, vec_spec, vec_spec, col_spec, row_spec, col_spec, col_spec, row_spec, table_spec, table_spec)
    out_specs = (act_spec, act_spec, col_spec, row_spec, col_spec, col_spec, row_spec)
    return jax.shard_map(layer_impl, mesh=mesh, in_specs=in_specs, out_specs=out_specs, check_vma=False)
```

time: 2500 us -> 2080 us (0.83)
  Pallas kernels: 0 us -> 1180 us
  matrix products: 1040 us -> 0 us
  waiting for transfers between devices: 1260 us -> 786 us
  other arithmetic: 171 us -> 10.8 us
  starting transfers between devices: 1.1 us -> 58.1 us
    pallas_call x0 -> x39, Pallas kernels: none -> 1180 us  [the longest x9 377 us: proj_call(): scalar_call(functools.partial(proj_kernel, ws, dims, len(extra), epi), (n...]
    dot_general x21 -> x0, matrix products: 1040 us -> none  [the longest x1 116 us: layer_body(): jnp.einsum('bsd,df->bsf', h_mlp_full, up_full, preferred_element_type=jnp...]
    reduce_scatter x9 -> x0, waiting for transfers between devices: 799 us -> none  [the longest x1 286 us: layer_body(): lax.psum_scatter(jnp.einsum('bsd,bsf->df', h_mlp_full, d_up, preferred_el...]
    ppermute x0 -> x46, waiting for transfers between devices: none -> 786 us  [the longest x21 520 us: px(): return lax.ppermute(v, 'fsdp', SWAP)]
    all_gather x9 -> x4, waiting for transfers between devices: 457 us -> 0.01 us  [both(): return lax.all_gather(v, 'model', axis=0, tiled=True)]
    convert_element_type x7 -> x0, other arithmetic: 79.4 us -> none  [the longest x1 20.2 us: layer_body(): d_mid = (grad_out.astype(jnp.float32) + d_mid_norm).astype(jnp.bfloat16)]
    reduce_sum x5 -> x0, other arithmetic: 59.4 us -> none  [the longest x1 26.8 us: attention_core(): attn_probs = jax.nn.softmax(scores, axis=-1).astype(jnp.bfloat16)]
    ppermute x0 -> x46, starting transfers between devices: none -> 48.2 us  [the longest x21 25.4 us: py(): return lax.ppermute(v, 'data', SWAP)]
  transfers between devices with their start and end apart: 18 -> 50, of which waited for: 14 -> 14; matrix products, arithmetic and copies ran while one was open for 28% -> 1% of each run, Pallas kernels for 0% -> 45%
where the time goes in v1:
time: 2080 us; the launch traced here: 2070 us
  Pallas kernels  1180 us (57%)
  waiting for transfers between devices  786 us (38%)
  starting transfers between devices  58.1 us (3%)
  local copies, waits for them, and re-layouts  22.3 us (1%)
    ppermute x21, waiting for transfers between devices, px(): return lax.ppermute(v, 'fsdp', SWAP)  520 us
    pallas_call x9, Pallas kernels, proj_call(): scalar_call(functools.partial(proj_kernel, ws, dims, len(extra), epi), (n...  377 us
    pallas_call x22, Pallas kernels, tn_call(): scalar_call(functools.partial(tn_kernel, len(adds)), (no, nb), [a_spec, b...  368 us
    ppermute x21, waiting for transfers between devices, py(): return lax.ppermute(v, 'data', SWAP)  252 us
    pallas_call x2, Pallas kernels, mlp_call(): scalar_call(functools.partial(mlp_kernel, ws, nc), (t // tile,), [row(d),...  248 us
    pallas_call x1, Pallas kernels, attn_bwd_call(): pl.pallas_call(functools.partial(attn_bwd_kernel, nb, seq), grid=(batch /...  61.5 us
    pallas_call x2, Pallas kernels, tn2_call(): scalar_call(functools.partial(tn2_kernel, len(adds), half), (n,), [pl.Blo...  57.7 us
  transfers between devices with their start and end apart: 50, of which 14 were waited for; matrix products, arithmetic and copies ran while one was open for 1% of the time, Pallas kernels for 45%

profile of v1, /device:TPU:0, one launch (start us, length us, event | category | flops | bytes accessed | tf_op | source)
XLA Modules:
  0.0 2074.2 jit_solution(4435727438181037465)
XLA Ops:
  23.7 33.4 %collective-permute-done.refs_1_.refs_2_.refs_6_ = bf16[512,1536]{1,0:T(8,128)(2,1)S(1)} collective-permute-done((bf16[512,1536]{1,0:T(8,128)(2,1)}, bf16[512,1536]{1,0:T(8,128)(2,1)S(1)}, u32[]{:S(2)}, u32[]{:S(2)}) %collective-permute-start) | collective-permute-done | bytes 1572896 | tf_op jit(solution)/shard_map/ppermute | solution.py:412
  98.5 37.9 %shard_map.163 = bf16[4096,1536]{1,0:T(8,128)(2,1)} custom-call(s32[6]{0:T(128)} %stack.27.ids, bf16[4096,2048]{1,0:T(8,128)(2,1)} %all-gather.5.cloned.1.call-done.h_ref.a_ref, f32[2,64,384]{2,1,0:T(8,128)} %bitcast.36, f32[2,64,384]{2,1,0:T(8,128)} %bitcast.38, bf16[512,1536]{1,0:T(8,128)(2,1)} %refs_5_.1, bf16[512,1536]{1,0:T(8,128)(2,1)} %copy-done.5, ...), custom_call_target="tpu_custom_call" | custom-call | flops 25769803776 | bytes 35651584 | tf_op jit(solution)/shard_map/pallas_call | solution.py:129
  136.5 22.4 %shard_map.164 = bf16[2,32,64,1024]{3,2,1,0:T(8,128)(2,1)} custom-call(bf16[2,32,64,1536]{3,2,1,0:T(8,128)(2,1)} %bitcast.44), custom_call_target="tpu_custom_call" | custom-call | flops 8000000000 | bytes 20000000 | tf_op jit(solution)/shard_map/pallas_call | solution.py:180
  188.0 22.4 %shard_map.166 = (bf16[2048,2048]{1,0:T(8,128)(2,1)}, bf16[2048,2048]{1,0:T(8,128)(2,1)}) custom-call(s32[6]{0:T(128)} %stack.27.ids, bf16[4096,1024]{1,0:T(8,128)(2,1)} %bitcast.25, bf16[2048,2048]{1,0:T(8,128)(2,1)} %collective-permute-done.8.refs_1_, bf16[2048,2048]{1,0:T(8,128)(2,1)} %bitcast.31, f32[1,2048]{1,0:T(1,128)} %bitcast.42, ...), custom_call_target="tpu_custom_call" | custom-call | flops 8589934592 | bytes 50331648 | tf_op jit(solution)/shard_map/pallas_call | solution.py:303
  234.4 130.3 %collective-permute-done.13.refs_6_.refs_3_.refs_5_ = bf16[2048,512]{1,0:T(8,128)(2,1)S(1)} collective-permute-done((bf16[2048,512]{1,0:T(8,128)(2,1)S(1)}, bf16[2048,512]{1,0:T(8,128)(2,1)S(1)}, u32[]{:S(2)}, u32[]{:S(2)}) %collective-permute-start.13) | collective-permute-done | bytes 2097184 | tf_op jit(solution)/shard_map/ppermute | solution.py:412
  369.4 85.5 %collective-permute-done.14.refs_7_.refs_4_.refs_6_ = bf16[2048,512]{1,0:T(8,128)(2,1)S(1)} collective-permute-done((bf16[2048,512]{1,0:T(8,128)(2,1)S(1)}, bf16[2048,512]{1,0:T(8,128)(2,1)S(1)}, u32[]{:S(2)}, u32[]{:S(2)}) %collective-permute-start.14) | collective-permute-done | bytes 2097184 | tf_op jit(solution)/shard_map/ppermute | solution.py:416
  456.7 41.9 %collective-permute-done.21.refs_6_.refs_8_.refs_10_ = bf16[2048,512]{1,0:T(8,128)(2,1)S(1)} collective-permute-done((bf16[2048,512]{1,0:T(8,128)(2,1)S(1)}, bf16[2048,512]{1,0:T(8,128)(2,1)S(1)}, u32[]{:S(2)}, u32[]{:S(2)}) %collective-permute-start.21) | collective-permute-done | bytes 2097184 | tf_op jit(solution)/shard_map/ppermute | solution.py:412
  506.9 60.3 %collective-permute-done.15.refs_8_.refs_5_.refs_7_ = bf16[1024,512]{1,0:T(8,128)(2,1)S(1)} collective-permute-done((bf16[1024,512]{1,0:T(8,128)(2,1)S(1)}, bf16[1024,512]{1,0:T(8,128)(2,1)S(1)}, u32[]{:S(2)}, u32[]{:S(2)}) %collective-permute-start.15) | collective-permute-done | bytes 1048608 | tf_op jit(solution)/shard_map/ppermute | solution.py:416
  571.8 123.9 %shard_map.167 = (bf16[4096,2048]{1,0:T(8,128)(2,1)}, bf16[4096,4096]{1,0:T(8,128)(2,1)}) custom-call(s32[6]{0:T(128)} %stack.27.ids, bf16[4096,2048]{1,0:T(8,128)(2,1)} %all-gather.7.cloned.1.call-done.h_ref.a_ref, bf16[4096,2048]{1,0:T(8,128)(2,1)} %all-gather.9.cloned.1.call-done.g_ref.b_ref, bf16[512,4096]{1,0:T(8,128)(2,1)} %copy-done.3, ...), custom_call_target="tpu_custom_call" | custom-call | flops 103079215104 | bytes 109051904 | tf_op jit(solution)/shard_map/pallas_call | solution.py:253
  695.8 124.0 %shard_map.168 = (bf16[4096,2048]{1,0:T(8,128)(2,1)}, bf16[4096,4096]{1,0:T(8,128)(2,1)}) custom-call(s32[6]{0:T(128)} %stack.27.ids, bf16[4096,2048]{1,0:T(8,128)(2,1)} %all-gather.7.cloned.1.call-done.h_ref.a_ref, bf16[4096,2048]{1,0:T(8,128)(2,1)} %all-gather.9.cloned.1.call-done.g_ref.b_ref, bf16[512,4096]{1,0:T(8,128)(2,1)} %copy-done.4, ...), custom_call_target="tpu_custom_call" | custom-call | flops 103079215104 | bytes 109051904 | tf_op jit(solution)/shard_map/pallas_call | solution.py:253
  819.8 81.8 %shard_map.171 = bf16[2048,2048]{1,0:T(8,128)(2,1)} custom-call(s32[6]{0:T(128)} %stack.27.ids, bf16[4096,4096]{1,0:T(8,128)(2,1)} %get-tuple-element.21.refs_0_.b_ref, bf16[4096,4096]{1,0:T(8,128)(2,1)} %get-tuple-element.22.refs_1_.b_ref, bf16[512,4096]{1,0:T(8,128)(2,1)} %copy-done.3, bf16[512,4096]{1,0:T(8,128)(2,1)} %copy-done.10, ...), custom_call_target="tpu_custom_call" | custom-call | flops 68719476736 | bytes 75497472 | tf_op jit(solution)/shard_map/pallas_call | solution.py:303
  901.6 24.7 %shard_map.186 = f32[512,4096]{1,0:T(8,128)} custom-call(s32[6]{0:T(128)} %stack.27.ids, bf16[4096,2048]{1,0:T(8,128)(2,1)} %all-gather.7.cloned.1.call-done.h_ref.a_ref, bf16[4096,4096]{1,0:T(8,128)(2,1)} %get-tuple-element.22.refs_1_.b_ref), custom_call_target="tpu_custom_call" | custom-call | flops 17179869184 | bytes 46137344 | tf_op jit(solution)/shard_map/pallas_call | solution.py:372
  942.6 90.1 %shard_map.172.refs_3_ = bf16[2048,2048]{1,0:T(8,128)(2,1)} custom-call(s32[6]{0:T(128)} %stack.27.ids, bf16[4096,4096]{1,0:T(8,128)(2,1)} %get-tuple-element.21.refs_0_.b_ref, bf16[4096,4096]{1,0:T(8,128)(2,1)} %get-tuple-element.22.refs_1_.b_ref, bf16[2048,2048]{1,0:T(8,128)(2,1)} %collective-permute-done.26.refs_2_, ...), custom_call_target="tpu_custom_call" | custom-call | flops 68719476736 | bytes 109051904 | tf_op jit(solution)/shard_map/pallas_call | solution.py:303
  1032.7 16.8 shard_map.196
  1067.6 24.7 %shard_map.189 = f32[512,4096]{1,0:T(8,128)} custom-call(s32[6]{0:T(128)} %stack.27.ids, bf16[4096,2048]{1,0:T(8,128)(2,1)} %all-gather.7.cloned.1.call-done.h_ref.a_ref, bf16[4096,4096]{1,0:T(8,128)(2,1)} %get-tuple-element.21.refs_0_.b_ref), custom_call_target="tpu_custom_call" | custom-call | flops 17179869184 | bytes 46137344 | tf_op jit(solution)/shard_map/pallas_call | solution.py:372
  1093.7 24.7 %shard_map.185 = f32[512,4096]{1,0:T(8,128)} custom-call(s32[6]{0:T(128)} %stack.27.ids, bf16[4096,2048]{1,0:T(8,128)(2,1)} %all-gather.7.cloned.1.call-done.h_ref.a_ref, bf16[4096,4096]{1,0:T(8,128)(2,1)} %get-tuple-element.22.refs_1_.b_ref), custom_call_target="tpu_custom_call" | custom-call | flops 17179869184 | bytes 46137344 | tf_op jit(solution)/shard_map/pallas_call | solution.py:372
  1149.4 139.9 %collective-permute-done.44.refs_0_ = f32[2048,512]{1,0:T(8,128)} collective-permute-done((f32[2048,512]{1,0:T(8,128)}, f32[2048,512]{1,0:T(8,128)}, u32[]{:S(2)}, u32[]{:S(2)}) %collective-permute-start.44) | collective-permute-done | bytes 4194336 | tf_op jit(solution)/shard_map/ppermute | solution.py:412
  1306.3 24.7 %shard_map.188 = f32[512,4096]{1,0:T(8,128)} custom-call(s32[6]{0:T(128)} %stack.27.ids, bf16[4096,2048]{1,0:T(8,128)(2,1)} %all-gather.7.cloned.1.call-done.h_ref.a_ref, bf16[4096,4096]{1,0:T(8,128)(2,1)} %get-tuple-element.21.refs_0_.b_ref), custom_call_target="tpu_custom_call" | custom-call | flops 17179869184 | bytes 46137344 | tf_op jit(solution)/shard_map/pallas_call | solution.py:372
  1331.1 45.4 %shard_map.169 = bf16[2048,2048]{1,0:T(8,128)(2,1)} custom-call(s32[6]{0:T(128)} %stack.27.ids, bf16[4096,2048]{1,0:T(8,128)(2,1)} %get-tuple-element.18.refs_0_.a_ref, bf16[4096,2048]{1,0:T(8,128)(2,1)} %get-tuple-element.19.refs_1_.a_ref, bf16[2048,512]{1,0:T(8,128)(2,1)} %copy-done.9, bf16[2048,512]{1,0:T(8,128)(2,1)} %copy-done.13, ...), custom_call_target="tpu_custom_call" | custom-call | flops 34359738368 | bytes 41943040 | tf_op jit(solution)/shard_map/pallas_call | solution.py:303
  1376.4 78.2 %collective-permute-done.45.refs_1_ = f32[2048,512]{1,0:T(8,128)} collective-permute-done((f32[2048,512]{1,0:T(8,128)}, f32[2048,512]{1,0:T(8,128)}, u32[]{:S(2)}, u32[]{:S(2)}) %collective-permute-start.45) | collective-permute-done | bytes 4194336 | tf_op jit(solution)/shard_map/ppermute | solution.py:416
  1454.6 16.9 shard_map.199.refs_2_
  1490.0 25.6 %shard_map.187 = f32[512,4096]{1,0:T(8,128)} custom-call(s32[6]{0:T(128)} %stack.27.ids, bf16[4096,2048]{1,0:T(8,128)(2,1)} %all-gather.7.cloned.1.call-done.h_ref.a_ref, bf16[4096,4096]{1,0:T(8,128)(2,1)} %get-tuple-element.22.refs_1_.b_ref, f32[512,4096]{1,0:T(8,128)} %collective-permute-done.35.refs_0_), custom_call_target="tpu_custom_call" | custom-call | flops 17179869184 | bytes 54525952 | tf_op jit(solution)/shard_map/pallas_call | solution.py:372
  1516.1 25.6 %shard_map.190 = f32[512,4096]{1,0:T(8,128)} custom-call(s32[6]{0:T(128)} %stack.27.ids, bf16[4096,2048]{1,0:T(8,128)(2,1)} %all-gather.7.cloned.1.call-done.h_ref.a_ref, bf16[4096,4096]{1,0:T(8,128)(2,1)} %get-tuple-element.21.refs_0_.b_ref, f32[512,4096]{1,0:T(8,128)} %collective-permute-done.38.refs_0_), custom_call_target="tpu_custom_call" | custom-call | flops 17179869184 | bytes 54525952 | tf_op jit(solution)/shard_map/pallas_call | solution.py:372
  1543.3 26.7 %shard_map.173 = bf16[4096,1024]{1,0:T(8,128)(2,1)} custom-call(s32[6]{0:T(128)} %stack.27.ids, bf16[4096,2048]{1,0:T(8,128)(2,1)} %all-gather.11.cloned.1.call-done.refs_0_.b_ref, bf16[1024,512]{1,0:T(8,128)(2,1)} %refs_1_.4, bf16[1024,512]{1,0:T(8,128)(2,1)} %collective-permute-done.4.refs_2_.refs_5_, ...), custom_call_target="tpu_custom_call" | custom-call | flops 17179869184 | bytes 29360128 | tf_op jit(solution)/shard_map/pallas_call | solution.py:303
  1569.9 61.5 %shard_map.174 = bf16[2,32,64,1536]{3,2,1,0:T(8,128)(2,1)} custom-call(bf16[2,32,64,1536]{3,2,1,0:T(8,128)(2,1)} %bitcast.45, bf16[2,32,64,1024]{3,2,1,0:T(8,128)(2,1)} %bitcast.47, f32[2,64,384]{2,1,0:T(8,128)} %bitcast.37, f32[2,64,384]{2,1,0:T(8,128)} %bitcast.39), custom_call_target="tpu_custom_call" | custom-call | flops 20000000000 | bytes 40000000 | tf_op jit(solution)/shard_map/pallas_call | solution.py:217
  1644.2 20.7 shard_map.175
  1666.6 47.8 %shard_map.170 = bf16[2048,2048]{1,0:T(8,128)(2,1)} custom-call(s32[6]{0:T(128)} %stack.27.ids, bf16[4096,2048]{1,0:T(8,128)(2,1)} %get-tuple-element.18.refs_0_.a_ref, bf16[4096,2048]{1,0:T(8,128)(2,1)} %get-tuple-element.19.refs_1_.a_ref, bf16[2048,2048]{1,0:T(8,128)(2,1)} %collective-permute-done.25.refs_2_, ...), custom_call_target="tpu_custom_call" | custom-call | flops 34359738368 | bytes 58720256 | tf_op jit(solution)/shard_map/pallas_call | solution.py:303
  1724.2 110.2 %collective-permute-done.39.refs_1_ = f32[512,4096]{1,0:T(8,128)} collective-permute-done((f32[512,4096]{1,0:T(8,128)}, f32[512,4096]{1,0:T(8,128)}, u32[]{:S(2)}, u32[]{:S(2)}) %collective-permute-start.39) | collective-permute-done | bytes 8388640 | tf_op jit(solution)/shard_map/ppermute | solution.py:412
  1834.8 28.9 %shard_map.191 = (f32[512,4096]{1,0:T(8,128)}, f32[512,4096]{1,0:T(8,128)}) custom-call(s32[6]{0:T(128)} %stack.27.ids, bf16[4096,2048]{1,0:T(8,128)(2,1)} %all-gather.7.cloned.1.call-done.h_ref.a_ref, bf16[4096,4096]{1,0:T(8,128)(2,1)} %get-tuple-element.21.refs_0_.b_ref, f32[512,4096]{1,0:T(8,128)} %collective-permute-done.37.refs_0_, ...), custom_call_target="tpu_custom_call" | custom-call | flops 17179869184 | bytes 62914560 | tf_op jit(solution)/shard_map/pallas_call | solution.py:403
  1929.4 28.8 %shard_map.192 = (f32[512,4096]{1,0:T(8,128)}, f32[512,4096]{1,0:T(8,128)}) custom-call(s32[6]{0:T(128)} %stack.27.ids, bf16[4096,2048]{1,0:T(8,128)(2,1)} %all-gather.7.cloned.1.call-done.h_ref.a_ref, bf16[4096,4096]{1,0:T(8,128)(2,1)} %get-tuple-element.22.refs_1_.b_ref, ...), custom_call_target="tpu_custom_call", output_to_operand_aliasing={{0}: (5, {}), {1}: (6, {})} | custom-call | flops 17179869184 | bytes 62914560 | tf_op jit(solution)/shard_map/pallas_call | solution.py:403
  1980.9 50.3 %collective-permute-done.31 = f32[1024,512]{1,0:T(8,128)} collective-permute-done((f32[1024,512]{1,0:T(8,128)}, f32[1024,512]{1,0:T(8,128)}, u32[]{:S(2)}, u32[]{:S(2)}) %collective-permute-start.31) | collective-permute-done | bytes 2097184 | tf_op jit(solution)/shard_map/ppermute | solution.py:412
  2041.0 26.4 %shard_map.176 = bf16[2048,2048]{1,0:T(8,128)(2,1)} custom-call(s32[6]{0:T(128)} %stack.27.ids, bf16[4096,1536]{1,0:T(8,128)(2,1)} %bitcast.23, bf16[2048,2048]{1,0:T(8,128)(2,1)} %collective-permute-done.27.refs_1_, bf16[2048,2048]{1,0:T(8,128)(2,1)} %bitcast.32, bf16[2048,2048]{1,0:T(8,128)(2,1)} %shard_map.172.refs_3_, f32[1,2048]{1,0:T(1,128)} %bitcast.41, ...), custom_call_target="tpu_custom_call" | custom-call | flops 12884901888 | bytes 54525952 | tf_op jit(solution)/shard_map/pallas_call | solution.py:303
  (182 shorter events, 357.3 us)
Async XLA Ops:
  17.5 554.4 %all-gather.9.cloned.1.call-start = ((), (), s32[]{:S(2)}) async-start(), calls=%async_computation.2 | async-start | bytes 25165824 | tf_op jit(solution)/shard_map/all_gather | solution.py:455
  18.2 553.6 %all-gather.7.cloned.1.call-start = ((), (), s32[]{:S(2)}) async-start(), calls=%async_computation.1 | async-start | bytes 25165824 | tf_op jit(solution)/shard_map/all_gather | solution.py:455
  210.4 1332.8 %all-gather.11.cloned.1.call-start = ((), (), s32[]{:S(2)}) async-start(), calls=%async_computation.3 | async-start | bytes 25165824 | tf_op jit(solution)/shard_map/all_gather | solution.py:455
  226.3 139.9 %collective-permute-start.9 = (bf16[512,4096]{1,0:T(8,128)(2,1)S(1)}, bf16[512,4096]{1,0:T(8,128)(2,1)S(1)}, u32[]{:S(2)}, u32[]{:S(2)}) collective-permute-start(bf16[512,4096]{1,0:T(8,128)(2,1)S(1)} %pad_maximum_fusion.refs_0_.refs_2_.refs_6_), channel_id=1, source_target_pairs={{0,2},{2,0},{1,3},{3,1},{4,6},{6,4},{5,7},{7,5}} | collective-permute-start | bytes 12582920 | tf_op jit(solution)/shard_map/ppermute | solution.py:412
  226.6 140.3 %collective-permute-start.10 = (bf16[512,4096]{1,0:T(8,128)(2,1)S(1)}, bf16[512,4096]{1,0:T(8,128)(2,1)}, u32[]{:S(2)}, u32[]{:S(2)}) collective-permute-start(bf16[512,4096]{1,0:T(8,128)(2,1)S(1)} %pad_maximum_fusion.refs_0_.refs_2_.refs_6_), channel_id=1, source_target_pairs={{0,4},{4,0},{1,5},{5,1},{2,6},{6,2},{3,7},{7,3}} | collective-permute-start | bytes 12582920 | tf_op jit(solution)/shard_map/ppermute | solution.py:416
  230.3 134.4 %collective-permute-start.13 = (bf16[2048,512]{1,0:T(8,128)(2,1)S(1)}, bf16[2048,512]{1,0:T(8,128)(2,1)S(1)}, u32[]{:S(2)}, u32[]{:S(2)}) collective-permute-start(bf16[2048,512]{1,0:T(8,128)(2,1)S(1)} %get-tuple-element.28.refs_5_.refs_2_.refs_4_), channel_id=1, source_target_pairs={{0,2},{2,0},{1,3},{3,1},{4,6},{6,4},{5,7},{7,5}} | collective-permute-start | bytes 6291464 | tf_op jit(solution)/shard_map/ppermute | solution.py:412
  231.5 270.2 %collective-permute-start.17 = (bf16[512,4096]{1,0:T(8,128)(2,1)S(1)}, bf16[512,4096]{1,0:T(8,128)(2,1)S(1)}, u32[]{:S(2)}, u32[]{:S(2)}) collective-permute-start(bf16[512,4096]{1,0:T(8,128)(2,1)S(1)} %pad_maximum_fusion.1.refs_0_.refs_7_.refs_11_), channel_id=1, source_target_pairs={{0,2},{2,0},{1,3},{3,1},{4,6},{6,4},{5,7},{7,5}} | collective-permute-start | bytes 12582920 | tf_op jit(solution)/shard_map/ppermute | solution.py:412
  232.9 271.5 %collective-permute-start.18 = (bf16[512,4096]{1,0:T(8,128)(2,1)S(1)}, bf16[512,4096]{1,0:T(8,128)(2,1)S(1)}, u32[]{:S(2)}, u32[]{:S(2)}) collective-permute-start(bf16[512,4096]{1,0:T(8,128)(2,1)S(1)} %pad_maximum_fusion.1.refs_0_.refs_7_.refs_11_), channel_id=1, source_target_pairs={{0,4},{4,0},{1,5},{5,1},{2,6},{6,2},{3,7},{7,3}} | collective-permute-start | bytes 12582920 | tf_op jit(solution)/shard_map/ppermute | solution.py:416
  366.2 132.4 %collective-permute-start.21 = (bf16[2048,512]{1,0:T(8,128)(2,1)S(1)}, bf16[2048,512]{1,0:T(8,128)(2,1)S(1)}, u32[]{:S(2)}, u32[]{:S(2)}) collective-permute-start(bf16[2048,512]{1,0:T(8,128)(2,1)S(1)} %get-tuple-element.27.refs_5_.refs_7_.refs_9_), channel_id=1, source_target_pairs={{0,2},{2,0},{1,3},{3,1},{4,6},{6,4},{5,7},{7,5}} | collective-permute-start | bytes 6291464 | tf_op jit(solution)/shard_map/ppermute | solution.py:412
  366.9 133.0 %collective-permute-start.22 = (bf16[2048,512]{1,0:T(8,128)(2,1)S(1)}, bf16[2048,512]{1,0:T(8,128)(2,1)S(1)}, u32[]{:S(2)}, u32[]{:S(2)}) collective-permute-start(bf16[2048,512]{1,0:T(8,128)(2,1)S(1)} %get-tuple-element.27.refs_5_.refs_7_.refs_9_), channel_id=1, source_target_pairs={{0,4},{4,0},{1,5},{5,1},{2,6},{6,2},{3,7},{7,3}} | collective-permute-start | bytes 6291464 | tf_op jit(solution)/shard_map/ppermute | solution.py:416
  454.9 115.6 %collective-permute-start.11 = (bf16[512,2048]{1,0:T(8,128)(2,1)S(1)}, bf16[512,2048]{1,0:T(8,128)(2,1)S(1)}, u32[]{:S(2)}, u32[]{:S(2)}) collective-permute-start(bf16[512,2048]{1,0:T(8,128)(2,1)S(1)} %slice.76), channel_id=1, source_target_pairs={{0,4},{4,0},{1,5},{5,1},{2,6},{6,2},{3,7},{7,3}} | collective-permute-start | bytes 6291464 | tf_op jit(solution)/shard_map/ppermute | solution.py:416
  504.4 191.3 %collective-permute-start.23 = (bf16[1024,512]{1,0:T(8,128)(2,1)}, bf16[1024,512]{1,0:T(8,128)(2,1)}, u32[]{:S(2)}, u32[]{:S(2)}) collective-permute-start(bf16[1024,512]{1,0:T(8,128)(2,1)} %slice.82), channel_id=1, source_target_pairs={{0,4},{4,0},{1,5},{5,1},{2,6},{6,2},{3,7},{7,3}} | collective-permute-start | bytes 3145736 | tf_op jit(solution)/shard_map/ppermute | solution.py:416
  567.2 128.5 %collective-permute-start.24 = (bf16[1024,512]{1,0:T(8,128)(2,1)S(1)}, bf16[1024,512]{1,0:T(8,128)(2,1)}, u32[]{:S(2)}, u32[]{:S(2)}) collective-permute-start(bf16[1024,512]{1,0:T(8,128)(2,1)S(1)} %slice.83), channel_id=1, source_target_pairs={{0,2},{2,0},{1,3},{3,1},{4,6},{6,4},{5,7},{7,5}} | collective-permute-start | bytes 3145736 | tf_op jit(solution)/shard_map/ppermute | solution.py:412
  569.0 126.7 %collective-permute-start.19 = (bf16[512,2048]{1,0:T(8,128)(2,1)S(1)}, bf16[512,2048]{1,0:T(8,128)(2,1)}, u32[]{:S(2)}, u32[]{:S(2)}) collective-permute-start(bf16[512,2048]{1,0:T(8,128)(2,1)S(1)} %slice.80), channel_id=1, source_target_pairs={{0,4},{4,0},{1,5},{5,1},{2,6},{6,2},{3,7},{7,3}} | collective-permute-start | bytes 6291464 | tf_op jit(solution)/shard_map/ppermute | solution.py:416
  570.5 125.3 %collective-permute-start.20 = (bf16[512,2048]{1,0:T(8,128)(2,1)}, bf16[512,2048]{1,0:T(8,128)(2,1)}, u32[]{:S(2)}, u32[]{:S(2)}) collective-permute-start(bf16[512,2048]{1,0:T(8,128)(2,1)} %slice.81), channel_id=1, source_target_pairs={{0,2},{2,0},{1,3},{3,1},{4,6},{6,4},{5,7},{7,5}} | collective-permute-start | bytes 6291464 | tf_op jit(solution)/shard_map/ppermute | solution.py:412
  926.3 563.6 %collective-permute-start.35 = (f32[512,4096]{1,0:T(8,128)}, f32[512,4096]{1,0:T(8,128)}, u32[]{:S(2)}, u32[]{:S(2)}) collective-permute-start(f32[512,4096]{1,0:T(8,128)} %shard_map.186), channel_id=1, source_target_pairs={{0,2},{2,0},{1,3},{3,1},{4,6},{6,4},{5,7},{7,5}} | collective-permute-start | bytes 25165832 | tf_op jit(solution)/shard_map/ppermute | solution.py:412
  942.0 191.3 %collective-permute-start.41 = (f32[2048,512]{1,0:T(8,128)}, f32[2048,512]{1,0:T(8,128)}, u32[]{:S(2)}, u32[]{:S(2)}) collective-permute-start(f32[2048,512]{1,0:T(8,128)} %shard_map.194), channel_id=1, source_target_pairs={{0,4},{4,0},{1,5},{5,1},{2,6},{6,2},{3,7},{7,3}} | collective-permute-start | bytes 12582920 | tf_op jit(solution)/shard_map/ppermute | solution.py:416
  1049.5 256.3 %collective-permute-start.43 = (f32[2048,512]{1,0:T(8,128)}, f32[2048,512]{1,0:T(8,128)}, u32[]{:S(2)}, u32[]{:S(2)}) collective-permute-start(f32[2048,512]{1,0:T(8,128)} %shard_map.196), channel_id=1, source_target_pairs={{0,2},{2,0},{1,3},{3,1},{4,6},{6,4},{5,7},{7,5}} | collective-permute-start | bytes 12582920 | tf_op jit(solution)/shard_map/ppermute | solution.py:412
  1065.7 223.6 %collective-permute-start.44 = (f32[2048,512]{1,0:T(8,128)}, f32[2048,512]{1,0:T(8,128)}, u32[]{:S(2)}, u32[]{:S(2)}) collective-permute-start(f32[2048,512]{1,0:T(8,128)} %shard_map.197), channel_id=1, source_target_pairs={{0,2},{2,0},{1,3},{3,1},{4,6},{6,4},{5,7},{7,5}} | collective-permute-start | bytes 12582920 | tf_op jit(solution)/shard_map/ppermute | solution.py:412
  1092.3 423.8 %collective-permute-start.38 = (f32[512,4096]{1,0:T(8,128)}, f32[512,4096]{1,0:T(8,128)}, u32[]{:S(2)}, u32[]{:S(2)}) collective-permute-start(f32[512,4096]{1,0:T(8,128)} %shard_map.189), channel_id=1, source_target_pairs={{0,4},{4,0},{1,5},{5,1},{2,6},{6,2},{3,7},{7,3}} | collective-permute-start | bytes 25165832 | tf_op jit(solution)/shard_map/ppermute | solution.py:416
  1133.3 338.2 %collective-permute-start.40 = (f32[2048,512]{1,0:T(8,128)}, f32[2048,512]{1,0:T(8,128)}, u32[]{:S(2)}, u32[]{:S(2)}) collective-permute-start(f32[2048,512]{1,0:T(8,128)} %shard_map.193), channel_id=1, source_target_pairs={{0,4},{4,0},{1,5},{5,1},{2,6},{6,2},{3,7},{7,3}} | collective-permute-start | bytes 12582920 | tf_op jit(solution)/shard_map/ppermute | solution.py:416
  1289.3 182.6 %collective-permute-start.42 = (f32[2048,512]{1,0:T(8,128)}, f32[2048,512]{1,0:T(8,128)}, u32[]{:S(2)}, u32[]{:S(2)}) collective-permute-start(f32[2048,512]{1,0:T(8,128)} %shard_map.195), channel_id=1, source_target_pairs={{0,2},{2,0},{1,3},{3,1},{4,6},{6,4},{5,7},{7,5}} | collective-permute-start | bytes 12582920 | tf_op jit(solution)/shard_map/ppermute | solution.py:412
  1305.8 148.8 %collective-permute-start.45 = (f32[2048,512]{1,0:T(8,128)}, f32[2048,512]{1,0:T(8,128)}, u32[]{:S(2)}, u32[]{:S(2)}) collective-permute-start(f32[2048,512]{1,0:T(8,128)} %shard_map.198), channel_id=1, source_target_pairs={{0,4},{4,0},{1,5},{5,1},{2,6},{6,2},{3,7},{7,3}} | collective-permute-start | bytes 12582920 | tf_op jit(solution)/shard_map/ppermute | solution.py:416
  1454.6 210.3 %collective-permute-start.25 = (bf16[2048,2048]{1,0:T(8,128)(2,1)}, bf16[2048,2048]{1,0:T(8,128)(2,1)}, u32[]{:S(2)}, u32[]{:S(2)}) collective-permute-start(bf16[2048,2048]{1,0:T(8,128)(2,1)} %shard_map.169), channel_id=1, source_target_pairs={{0,1},{1,0},{2,3},{3,2},{4,5},{5,4},{6,7},{7,6}} | collective-permute-start | bytes 25165832 | tf_op jit(solution)/shard_map/ppermute | solution.py:420
  1471.5 457.0 %collective-permute-start.34 = (f32[512,4096]{1,0:T(8,128)}, f32[512,4096]{1,0:T(8,128)}, u32[]{:S(2)}, u32[]{:S(2)}) collective-permute-start(f32[512,4096]{1,0:T(8,128)} %shard_map.185), channel_id=1, source_target_pairs={{0,2},{2,0},{1,3},{3,1},{4,6},{6,4},{5,7},{7,5}} | collective-permute-start | bytes 25165832 | tf_op jit(solution)/shard_map/ppermute | solution.py:412
  1471.8 193.2 %collective-permute-start.37 = (f32[512,4096]{1,0:T(8,128)}, f32[512,4096]{1,0:T(8,128)}, u32[]{:S(2)}, u32[]{:S(2)}) collective-permute-start(f32[512,4096]{1,0:T(8,128)} %shard_map.188), channel_id=1, source_target_pairs={{0,4},{4,0},{1,5},{5,1},{2,6},{6,2},{3,7},{7,3}} | collective-permute-start | bytes 25165832 | tf_op jit(solution)/shard_map/ppermute | solution.py:416
  1515.6 413.4 %collective-permute-start.36 = (f32[512,4096]{1,0:T(8,128)}, f32[512,4096]{1,0:T(8,128)}, u32[]{:S(2)}, u32[]{:S(2)}) collective-permute-start(f32[512,4096]{1,0:T(8,128)} %shard_map.187), channel_id=1, source_target_pairs={{0,4},{4,0},{1,5},{5,1},{2,6},{6,2},{3,7},{7,3}} | collective-permute-start | bytes 25165832 | tf_op jit(solution)/shard_map/ppermute | solution.py:416
  1541.7 292.7 %collective-permute-start.39 = (f32[512,4096]{1,0:T(8,128)}, f32[512,4096]{1,0:T(8,128)}, u32[]{:S(2)}, u32[]{:S(2)}) collective-permute-start(f32[512,4096]{1,0:T(8,128)} %shard_map.190), channel_id=1, source_target_pairs={{0,2},{2,0},{1,3},{3,1},{4,6},{6,4},{5,7},{7,5}} | collective-permute-start | bytes 25165832 | tf_op jit(solution)/shard_map/ppermute | solution.py:412
  1664.9 376.1 %collective-permute-start.27 = (bf16[2048,2048]{1,0:T(8,128)(2,1)}, bf16[2048,2048]{1,0:T(8,128)(2,1)}, u32[]{:S(2)}, u32[]{:S(2)}) collective-permute-start(bf16[2048,2048]{1,0:T(8,128)(2,1)} %shard_map.175), channel_id=1, source_target_pairs={{0,1},{1,0},{2,3},{3,2},{4,5},{5,4},{6,7},{7,6}} | collective-permute-start | bytes 25165832 | tf_op jit(solution)/shard_map/ppermute | solution.py:420
  1665.0 236.9 %collective-permute-start.29 = (f32[512,1536]{1,0:T(8,128)S(1)}, f32[512,1536]{1,0:T(8,128)}, u32[]{:S(2)}, u32[]{:S(2)}) collective-permute-start(f32[512,1536]{1,0:T(8,128)S(1)} %copy-done.7), channel_id=1, source_target_pairs={{0,4},{4,0},{1,5},{5,1},{2,6},{6,2},{3,7},{7,3}} | collective-permute-start | bytes 9437192 | tf_op jit(solution)/shard_map/ppermute | solution.py:416
  1901.9 133.6 %collective-permute-start.28 = (f32[512,1536]{1,0:T(8,128)}, f32[512,1536]{1,0:T(8,128)}, u32[]{:S(2)}, u32[]{:S(2)}) collective-permute-start(f32[512,1536]{1,0:T(8,128)} %shard_map.178), channel_id=1, source_target_pairs={{0,4},{4,0},{1,5},{5,1},{2,6},{6,2},{3,7},{7,3}} | collective-permute-start | bytes 9437192 | tf_op jit(solution)/shard_map/ppermute | solution.py:416
  1916.8 118.7 %collective-permute-start.30 = (f32[512,1536]{1,0:T(8,128)}, f32[512,1536]{1,0:T(8,128)}, u32[]{:S(2)}, u32[]{:S(2)}) collective-permute-start(f32[512,1536]{1,0:T(8,128)} %shard_map.180), channel_id=1, source_target_pairs={{0,2},{2,0},{1,3},{3,1},{4,6},{6,4},{5,7},{7,5}} | collective-permute-start | bytes 9437192 | tf_op jit(solution)/shard_map/ppermute | solution.py:412
  (40 other events, 2156.5 us)
Sparse Core Ops, SparseCore 0:
  17.6 30.0 all-gather.4
  49.2 28.4 all-gather.8
  210.6 27.3 all-gather.6
  1032.8 27.9 all-gather.10
